TPU v7x, 256 devices: a whole 4x4x8 slice. The times are simulated.
256 devices in a mesh: dp: 32 (over x, z_hi, core), mp: 8 (over z_lo, y).
Axes of the slice: x: 4, y: 4, z: 8 (z_hi: 4, z_lo: 2; z = z_hi * 2 + z_lo), core: 2. Of those that a mesh axis runs over, the one named last changes fastest.
Arguments:
- tokens: bfloat16 [32, 2048, 2048], P('dp'), may hold values from -80 to 80
- w_query: bfloat16 [2048, 2048], P('dp', 'mp'), may hold values from -0.125 to 0.125
- w_key: bfloat16 [2048, 2048], P('dp', 'mp'), may hold values from -0.125 to 0.125
- w_value: bfloat16 [2048, 2048], P('dp', 'mp'), may hold values from -0.125 to 0.125
- w_out: bfloat16 [2048, 2048], P('mp', 'dp'), may hold values from -0.125 to 0.125
- memory: float32 [16, 128, 128], P('mp', 'dp'), may hold values from -3 to 3
- normalizer: float32 [16, 128], P('mp', 'dp'), may hold values from 0.02 to 0.2
- gate_bias: float32 [16], P('mp'), may hold values from -2 to 2
Outputs:
- output: bfloat16 [32, 2048, 2048], P('dp', None, 'mp')
- memory_new: float32 [16, 128, 128], P('mp', 'dp')
- normalizer_new: float32 [16, 128], P('mp', 'dp')
All inputs are finite; a program needn't handle non-finite values.
Results may differ from a plain program's by a relative error of at most 0.025.
Values may be sent and summed in bfloat16 or wider, within the bound.
A program may use at most 128 MiB of HBM per device.

v0:
```python
import math

import jax
import jax.numpy as jnp
from jax import lax
from jax.sharding import PartitionSpec as P


def in_one_piece(arrays, axis, dim, along):
    both = jnp.concatenate(arrays, axis=along)
    result, at, gathered = (lax.all_gather(both, axis, axis=dim, tiled=True), 0, [])
    for a in arrays:
        gathered.append(lax.slice_in_dim(result, at, at + a.shape[along], axis=along))
        at += a.shape[along]
    return tuple(gathered)


def in_one_piece_2(arrays, axis, dim, along):
    widths = [math.prod(a.shape[along:]) for a in arrays]
    both = jnp.concatenate(
        [a.reshape(*a.shape[:along], w) for a, w in zip(arrays, widths)], axis=along
    )
    result = lax.all_gather(both, axis, axis=dim, tiled=True)
    tiles = jnp.split(result, [sum(widths[:k]) for k in range(1, len(widths))], axis=along)
    return tuple(
        (b.reshape(*result.shape[:along], *a.shape[along:]) for a, b in zip(arrays, tiles))
    )


def split_up(x, dim, length):
    lengths = x.shape
    tiles = x.reshape(*lengths[:dim], length, lengths[dim] // length, *lengths[dim + 1 :])
    return jnp.moveaxis(tiles, dim, 0)


def sent_and_summed(x, axis, dim):
    length = lax.axis_size(axis)
    tiles = lax.all_to_all(split_up(x, dim, length), axis, 0, 0, tiled=True)
    return jnp.sum(tiles.astype(jnp.float32), axis=0)


def sent_together(arrays, axis, dim, along):
    widths = [math.prod(a.shape[along:]) for a in arrays]
    both = jnp.concatenate(
        [a.reshape(*a.shape[:along], w) for a, w in zip(arrays, widths)], axis=along
    )
    result = sent_and_summed(both, axis, dim)
    tiles = jnp.split(result, [sum(widths[:k]) for k in range(1, len(widths))], axis=along)
    return tuple(
        (b.reshape(*result.shape[:along], *a.shape[along:]) for a, b in zip(arrays, tiles))
    )


def feature_map(values):
    return jnp.where(values > 0, values + 1.0, jnp.exp(jnp.minimum(values, 0.0)))


def body(tokens, w_query, w_key, w_value, w_out, memory, normalizer, gate_bias):
    seq_count, seg_len, model_width = tokens.shape
    head_count = gate_bias.shape[0]
    proj_width = w_query.shape[1]
    head_dim = proj_width // head_count
    flat = tokens.reshape(seq_count * seg_len, model_width)

    def add_rows(piece):
        return jnp.dot(flat, piece, preferred_element_type=jnp.float32)

    pieces = in_one_piece((w_query, w_key, w_value), "dp", 0, 1)
    query_sum = add_rows(pieces[0])
    key_sum = add_rows(pieces[1])
    value_sum = add_rows(pieces[2])
    shape = (seq_count, seg_len, head_count, head_dim)
    query = query_sum.astype(jnp.bfloat16).reshape(shape)
    keys = key_sum.astype(jnp.bfloat16).reshape(shape)
    values = value_sum.astype(jnp.bfloat16).reshape(shape)
    whole_memory, whole_norm = in_one_piece_2((memory, normalizer), "dp", 1, 2)
    mixing = jax.nn.sigmoid(gate_bias)
    scale = 1.0 / math.sqrt(head_dim)
    block = min(512, seg_len)
    positions = jnp.arange(seg_len)
    query_seq = query[0]
    key_seq = keys[0]
    value_seq = values[0]
    feat_query = feature_map(query_seq.astype(jnp.float32))
    numer = jnp.einsum("thi,hij->thj", feat_query, whole_memory)
    denom = jnp.einsum("thi,hi->th", feat_query, whole_norm)
    retrieved = numer / denom[:, :, None]
    pieces = []
    for first in range(0, seg_len, block):
        last = first + block
        scores = (
            jnp.einsum(
                "qhd,khd->hqk",
                query_seq[first:last],
                key_seq[:last],
                preferred_element_type=jnp.float32,
            )
            * scale
        )
        allowed = positions[first:last, None] >= positions[None, :last]
        scores = jnp.where(allowed[None], scores, -1e30)
        probs = jax.nn.softmax(scores, axis=-1).astype(jnp.bfloat16)
        pieces.append(
            jnp.einsum("hqk,khd->qhd", probs, value_seq[:last], preferred_element_type=jnp.float32)
        )
    local = jnp.concatenate(pieces, axis=0)
    combined = (mixing[None, :, None] * retrieved + (1.0 - mixing)[None, :, None] * local).astype(
        jnp.bfloat16
    )
    combined_rows = combined.reshape(seg_len, proj_width)
    feat_key = feature_map(key_seq.astype(jnp.float32))
    key_numer = jnp.einsum("thi,hij->thj", feat_key, whole_memory)
    key_denom = jnp.einsum("thi,hi->th", feat_key, whole_norm)
    residual = value_seq.astype(jnp.float32) - key_numer / key_denom[:, :, None]
    delta_total = jnp.einsum("thi,thj->hij", feat_key, residual)
    key_total = jnp.sum(feat_key, axis=0)
    terms = jnp.dot(
        combined_rows,
        lax.all_gather(w_out, "dp", axis=1, tiled=True),
        preferred_element_type=jnp.float32,
    ).astype(jnp.bfloat16)
    summed = lax.psum_scatter(
        terms.astype(jnp.float32).astype(jnp.bfloat16), "mp", scatter_dimension=1, tiled=True
    ).astype(jnp.float32)
    output = summed.astype(jnp.bfloat16).reshape(seq_count, seg_len, summed.shape[1])
    batch_total = seq_count * lax.axis_size("dp")
    delta_part, key_part = sent_together(
        (delta_total.astype(jnp.bfloat16), key_total.astype(jnp.bfloat16)), "dp", 1, 2
    )
    memory_new = memory + delta_part / seg_len
    normalizer_new = normalizer + key_part / (seg_len * batch_total)
    return (output, memory_new, normalizer_new)


def solution(mesh):
    in_specs = (
        P("dp", None, None),
        P("dp", "mp"),
        P("dp", "mp"),
        P("dp", "mp"),
        P("mp", "dp"),
        P("mp", "dp", None),
        P("mp", "dp"),
        P("mp"),
    )
    out_specs = (P("dp", None, "mp"), P("mp", "dp", None), P("mp", "dp"))
    return jax.shard_map(body, mesh=mesh, in_specs=in_specs, out_specs=out_specs, check_vma=False)
```

profile of v0, /device:TPU:1, one launch (start us, length us, event | category | flops | bytes accessed | tf_op | source)
XLA Modules:
  0.0 238.3 jit_solution(2436392186417141879)
XLA Ops:
  7.2 0.0 all-gather.3.cloned.1.call-start
  7.2 1.4 pad_maximum_fusion
  8.7 0.0 all-gather.5.cloned.1.call-start
  8.7 0.7 all-gather.5.cloned.1.call-update
  9.4 0.0 reduce-scatter.2.cloned.1.call-start
  9.5 0.8 copy.74
  10.3 0.7 copy.73
  11.0 49.1 %all_gather.9 = bf16[2,128,129]{2,0,1:T(2,128)(2,1)S(1)} all-gather(bf16[2,4,129]{2,0,1:T(2,128)(2,1)S(1)} %pad_maximum_fusion.1), channel_id=1, replica_groups=mesh['dp'=32,'mp'=8] {'dp'}, dimensions={1}, use_global_device_ids=true | all-gather | bytes 68112 | tf_op jit(solution)/shard_map/all_gather | solution.py:23
  60.2 0.1 copy.107
  60.3 0.7 iota_compare_fusion
  61.0 0.2 broadcast_compare_fusion.2
  61.2 0.1 copy.92
  61.3 1.4 broadcast_compare_fusion
  62.7 1.2 broadcast_compare_fusion.1
  63.9 8.1 %all-gather.3.cloned.1.call-done = bf16[2048,768]{1,0:T(8,128)(2,1)} async-done(((bf16[64,768]{1,0:T(8,128)(2,1)}), bf16[2048,768]{1,0:T(8,128)(2,1)}) %all-gather.3.cloned.1.call-update) | async-done | bytes 3145744 | tf_op jit(solution)/shard_map/all_gather | solution.py:11
  72.0 6.2 %fusion.30 = bf16[256,2048]{1,0:T(8,128)(2,1)S(1)} fusion(bf16[1,2048,2048]{2,1,0:T(8,128)(2,1)} %param.8, bf16[2048,768]{1,0:T(8,128)(2,1)} %all-gather.3.cloned.1.call-done), kind=kOutput, calls=%fused_computation.50 | convolution fusion | flops 2148007936 | bytes 10485760 | tf_op jit(solution)/shard_map/dot_general | solution.py:66
  78.3 0.9 slice.126
  79.2 0.9 slice.123
  80.1 6.8 %fusion.44 = (bf16[256]{0:T(256)(128)(2,1)S(1)}, bf16[256,2048]{1,0:T(8,128)(2,1)S(1)}) fusion(bf16[1,2048,2048]{2,1,0:T(8,128)(2,1)} %param.8, bf16[2048,768]{1,0:T(8,128)(2,1)S(1)} %copy-done.5), kind=kOutput, calls=%fused_computation.58 | convolution fusion | flops 2151153408 | bytes 10486272 | tf_op jit(solution)/shard_map/dot_general | solution.py:66
  86.9 0.9 slice.128
  87.8 0.9 slice.125
  88.7 0.7 slice.119
  89.4 0.7 slice.122
  90.2 2.7 %fusion.39 = (bf16[2048,256]{0,1:T(8,128)(2,1)S(1)}, bf16[2048,256]{0,1:T(8,128)(2,1)S(1)}) fusion(bf16[1,2048,2048]{2,1,0:T(8,128)(2,1)S(1)} %bitcast.145, bf16[2048,768]{1,0:T(8,128)(2,1)S(1)} %copy-done.5), kind=kOutput, calls=%fused_computation.53 | convolution fusion | flops 2150629376 | bytes 11534336 | tf_op jit(solution)/shard_map/dot_general | solution.py:66
  92.9 1.1 fusion.113
  94.0 0.2 copy-done
  94.2 0.2 fusion.118
  94.4 4.1 %fusion.115 = f32[2,512]{1,0:T(2,128)S(1)} fusion(pred[512,1536]{1,0:T(8,128)(4,1)} %broadcast_compare_fusion, bf16[512,2,128]{0,2,1:T(8,128)(2,1)} %bitcast.138, bf16[1536,2,128]{0,2,1:T(8,128)(2,1)} %bitcast.127), kind=kOutput, calls=%fused_computation.132 | convolution fusion | flops 408946176 | bytes 1839104 | tf_op jit(solution)/shard_map/sub | solution.py:102
  98.5 5.3 %fusion.59 = f32[512,2,128]{0,2,1:T(8,128)} fusion(bf16[1536,2,128]{0,2,1:T(8,128)(2,1)} %bitcast.126, f32[2,512]{1,0:T(2,128)S(1)} %fusion.115, pred[512,1536]{1,0:T(8,128)(4,1)} %broadcast_compare_fusion, bf16[512,2,128]{0,2,1:T(8,128)(2,1)} %bitcast.139, bf16[1536,2,128]{0,2,1:T(8,128)(2,1)} %bitcast.128), kind=kOutput, calls=%fused_computation.74 | convolution fusion | flops 813173248 | bytes 3149824 | tf_op jit(solution)/shard_map/hqk,khd->qhd/dot_general | solution.py:104
  103.9 2.0 fusion.117
  105.9 3.2 %convolution_bitcast_fusion.2 = f32[512,2,128]{0,2,1:T(8,128)} fusion(bf16[512,2,128]{0,2,1:T(8,128)(2,1)} %bitcast.131, f32[2,512]{1,0:T(2,128)S(1)} %fusion.117, pred[512,512]{0,1:T(8,128)(4,1)S(1)} %broadcast_compare_fusion.2, bf16[512,2,128]{0,2,1:T(8,128)(2,1)} %bitcast.137, bf16[512,2,128]{0,2,1:T(8,128)(2,1)} %bitcast.133), kind=kOutput, calls=%fused_computation.73 | convolution fusion | flops 271058432 | bytes 1576960 | tf_op jit(solution)/shard_map/hqk,khd->qhd/dot_general | solution.py:104
  109.1 4.9 %fusion.116 = (f32[2,512]{1,0:T(2,128)S(1)}, f32[2,512,1024]{2,1,0:T(8,128)}) fusion(pred[512,1024]{1,0:T(8,128)(4,1)} %broadcast_compare_fusion.1, bf16[512,2,128]{0,2,1:T(8,128)(2,1)} %bitcast.135, bf16[1024,2,128]{0,2,1:T(8,128)(2,1)} %bitcast.130), kind=kOutput, calls=%fused_computation.133 | convolution fusion | flops 272630784 | bytes 5509120 | tf_op jit(solution)/shard_map/sub | solution.py:102
  114.0 4.1 %fusion.58 = f32[512,2,128]{0,2,1:T(8,128)} fusion(bf16[1024,2,128]{0,2,1:T(8,128)(2,1)} %bitcast.129, f32[2,512,1024]{2,1,0:T(8,128)} %get-tuple-element.14, f32[2,512]{1,0:T(2,128)S(1)} %get-tuple-element.13), kind=kOutput, calls=%fused_computation.72 | convolution fusion | flops 270532608 | bytes 5246976 | tf_op jit(solution)/shard_map/hqk,khd->qhd/dot_general | solution.py:104
  118.1 5.2 %fusion.114 = (f32[2,512]{1,0:T(2,128)S(1)}, f32[2,512,2048]{2,1,0:T(8,128)}) fusion(pred[512,2048]{1,0:T(8,128)(4,1)S(1)} %iota_compare_fusion, bf16[512,2,128]{0,2,1:T(8,128)(2,1)S(1)} %bitcast.134, bf16[2048,2,128]{0,2,1:T(8,128)(2,1)S(1)} %bitcast.120), kind=kOutput, calls=%fused_computation.131 | convolution fusion | flops 545261568 | bytes 10752000 | tf_op jit(solution)/shard_map/sub | solution.py:102
  123.3 5.1 %fusion.60 = f32[512,2,128]{0,2,1:T(8,128)S(1)} fusion(bf16[2048,2,128]{0,2,1:T(8,128)(2,1)S(1)} %bitcast.115, f32[2,512,2048]{2,1,0:T(8,128)} %get-tuple-element.12, f32[2,512]{1,0:T(2,128)S(1)} %get-tuple-element.11), kind=kOutput, calls=%fused_computation.75 | convolution fusion | flops 541065216 | bytes 9965568 | tf_op jit(solution)/shard_map/hqk,khd->qhd/dot_general | solution.py:104
  128.5 0.5 fusion.26
  129.0 6.9 %convolution_convert_fusion = bf16[2048,2048]{1,0:T(8,128)(2,1)} fusion(bf16[2048,256]{0,1:T(8,128)(2,1)S(1)} %bitcast.123, bf16[256,2048]{0,1:T(8,128)(2,1)} %all-gather.5.cloned.1.call-done), kind=kOutput, calls=%fused_computation.13 | convolution fusion | flops 2151677952 | bytes 10485760 | tf_op jit(solution)/shard_map/dot_general | solution.py:117
  135.9 0.1 convert_element_type.91
  136.0 0.5 copy.90
  136.5 0.6 fusion.52
  137.2 1.4 fusion.61
  138.6 0.1 maximum_bitcast_fusion
  138.7 18.5 %all_to_all.5 = bf16[32,2,4,129]{3,2,1,0:T(4,128)(2,1)S(1)} all-to-all(bf16[32,2,4,129]{3,2,1,0:T(4,128)(2,1)S(1)} %maximum_bitcast_fusion), channel_id=1, replica_groups=mesh['dp'=32,'mp'=8] {'dp'}, dimensions={0} | all-to-all | bytes 132096 | tf_op jit(solution)/shard_map/all_to_all | solution.py:38
  157.2 0.1 convert_reduce_fusion
  157.3 0.1 fusion.87
  157.4 0.6 add.30
  157.9 0.6 fusion.88
  158.5 73.2 %reduce-scatter.2.cloned.1.call-done = bf16[2048,256]{1,0:T(8,128)(2,1)} async-done(((bf16[2048,2048]{1,0:T(8,128)(2,1)}), bf16[2048,256]{1,0:T(8,128)(2,1)}) %reduce-scatter.2.cloned.1.call-update) | async-done | bytes 1048592 | tf_op jit(solution)/shard_map/reduce_scatter | solution.py:122
  (39 shorter events, 0.3 us)
Async XLA Ops:
  7.2 54.0 %copy-start.6 = (f32[2]{0:T(128)S(1)}, f32[2]{0:T(128)}, u32[]{:S(2)}) copy-start(f32[2]{0:T(128)} %param.15) | copy-start | bytes 28
  7.2 64.9 %all-gather.3.cloned.1.call-start = ((), (), s32[]{:S(2)}) async-start(), calls=%async_computation.2 | async-start | bytes 3244032 | tf_op jit(solution)/shard_map/all_gather | solution.py:11
  8.7 120.3 %all-gather.5.cloned.1.call-start = ((), (), s32[]{:S(2)}) async-start(), calls=%async_computation.3 | async-start | bytes 1081344 | tf_op jit(solution)/shard_map/all_gather | solution.py:119
  9.4 222.3 %reduce-scatter.2.cloned.1.call-start = ((), (), s32[]{:S(2)}) async-start(), calls=%async_computation.4 | async-start | bytes 9437184 | tf_op jit(solution)/shard_map/reduce_scatter | solution.py:122
  72.0 8.1 %copy-start.5 = (bf16[2048,768]{1,0:T(8,128)(2,1)S(1)}, bf16[2048,768]{1,0:T(8,128)(2,1)}, u32[]{:S(2)}) copy-start(bf16[2048,768]{1,0:T(8,128)(2,1)} %all-gather.3.cloned.1.call-done) | copy-start | bytes 9437188
  79.2 10.9 %slice-start = ((s8[8388608]{0:T(1024)(128)(4,1)}), s8[4194304]{0:T(1024)(128)(4,1)S(1)}, s32[]{:S(2)}) async-start(s8[8388608]{0:T(1024)(128)(4,1)} %bitcast.144), calls=%async_computation.5 | async-start | bytes 8388608
  80.1 10.1 %slice-start.1 = ((s8[8388608]{0:T(1024)(128)(4,1)}), s8[4194304]{0:T(1024)(128)(4,1)S(1)}, s32[]{:S(2)}) async-start(s8[8388608]{0:T(1024)(128)(4,1)} %bitcast.144), calls=%async_computation.6 | async-start | bytes 8388608
  92.9 1.3 copy-start
  114.0 4.1 %copy-start.2 = (bf16[512,256]{0,1:T(8,128)(2,1)S(1)}, bf16[512,256]{0,1:T(8,128)(2,1)}, u32[]{:S(2)}) copy-start(bf16[512,256]{0,1:T(8,128)(2,1)} %get-tuple-element.6) | copy-start | bytes 786436
  123.3 5.2 %copy-start.1 = (bf16[2048,256]{0,1:T(8,128)(2,1)S(1)}, bf16[2048,256]{0,1:T(8,128)(2,1)}, u32[]{:S(2)}) copy-start(bf16[2048,256]{0,1:T(8,128)(2,1)} %copy-done) | copy-start | bytes 3145732
  123.3 5.2 %copy-start.7 = (f32[512,2,128]{0,2,1:T(8,128)S(1)}, f32[512,2,128]{0,2,1:T(8,128)}, u32[]{:S(2)}) copy-start(f32[512,2,128]{0,2,1:T(8,128)} %convolution_bitcast_fusion.2) | copy-start | bytes 1572868
  123.3 5.2 %copy-start.8 = (f32[512,2,128]{0,2,1:T(8,128)S(1)}, f32[512,2,128]{0,2,1:T(8,128)}, u32[]{:S(2)}) copy-start(f32[512,2,128]{0,2,1:T(8,128)} %fusion.59) | copy-start | bytes 1572868
  123.3 5.2 %copy-start.9 = (f32[512,2,128]{0,2,1:T(8,128)S(1)}, f32[512,2,128]{0,2,1:T(8,128)}, u32[]{:S(2)}) copy-start(f32[512,2,128]{0,2,1:T(8,128)} %fusion.58) | copy-start | bytes 1572868
  137.2 20.2 %copy-start.4 = (f32[2,4]{1,0:T(2,128)S(1)}, f32[2,4]{1,0:T(2,128)}, u32[]{:S(2)}) copy-start(f32[2,4]{1,0:T(2,128)} %param.14) | copy-start | bytes 100
  137.2 20.7 %copy-start.3 = (f32[2,4,128]{2,1,0:T(4,128)S(1)}, f32[2,4,128]{2,1,0:T(4,128)}, u32[]{:S(2)}) copy-start(f32[2,4,128]{2,1,0:T(4,128)} %param.13) | copy-start | bytes 12292
Sparse Core Ops, SparseCore 0:
  11.1 60.8 all-gather.2
  74.6 50.0 all-gather.4
  136.0 95.6 reduce-scatter.1
where the time goes:
time: 239 us; the launch traced here: 238 us
  waiting for transfers between devices  82.1 us (34%)
  blocking collectives  67.6 us (28%)
  matrix products  59.3 us (25%)
  between operations  14 us (6%)
  local copies, waits for them, and re-layouts  8.84 us (4%)
  other arithmetic  6.33 us (3%)
    reduce_scatter x1, waiting for transfers between devices, body(): lax.psum_scatter(terms.astype(jnp.float32).astype(jnp.bfloat16), 'mp', sc...  73.2 us
    all_gather x1, blocking collectives, in_one_piece_2(): result = lax.all_gather(both, axis, axis=dim, tiled=True)  49.1 us
    all_to_all x1, blocking collectives, sent_and_summed(): tiles = lax.all_to_all(split_up(x, dim, length), axis, 0, 0, tiled=True)  18.5 us
    dot_general x4, matrix products, body(): jnp.einsum('hqk,khd->qhd', probs, value_seq[:last], preferred_element_typ...  17.8 us
    sub x4, matrix products, body(): probs = jax.nn.softmax(scores, axis=-1).astype(jnp.bfloat16)  16.2 us
    dot_general x3, matrix products, add_rows(): return jnp.dot(flat, piece, preferred_element_type=jnp.float32)  15.7 us
    all_gather x1, waiting for transfers between devices, in_one_piece(): lax.all_gather(both, axis, axis=dim, tiled=True)  8.14 us
    dot_general x1, matrix products, body(): jnp.dot(combined_rows, lax.all_gather(w_out, 'dp', axis=1, tiled=True), p...  6.86 us
  transfers between devices with their start and end apart: 3, of which 2 were waited for; matrix products, arithmetic and copies ran while one was open for 28% of the time, Pallas kernels for 0%

commit v1 on v0

v1 whole, which is shorter than its diff:
```python
import functools
import math

import jax
import jax.numpy as jnp
from jax import lax
from jax.experimental import pallas as pl
from jax.experimental.pallas import tpu as pltpu
from jax.sharding import PartitionSpec as P

MESH = pl.DeviceIdType.MESH
F32, BF16 = jnp.float32, jnp.bfloat16

NX, NZH, NC = 4, 4, 2
NZL, NY = 2, 4
DP, MP = NX * NZH * NC, NZL * NY
SEG, D, HD, HW = 2048, 2048, 128, 256
SH = D // DP
PW = 4 * HW
CH = 256
NCH = SEG // CH
SCALE2 = math.log2(math.e) / math.sqrt(HD)

ZF, L0, L1 = 144, 80, 208


def nt(a, b):
    return lax.dot_general(a, b, (((1,), (1,)), ((), ())), preferred_element_type=F32)


def nn(a, b):
    return jnp.dot(a, b, preferred_element_type=F32)


def feature(u):
    return jnp.where(u > 0, u + 1.0, jnp.exp(jnp.minimum(u, 0.0)))


def kernel(
    tok_hbm, wsh, memn, memf, normf, gate,
    out, mem_out, norm_out,
    tok, w, wo, keys, vals, gath, qs, scr, mx, acc, mm, memg, dacc, stage, drecv,
    tok_sem, ws_sem, wz_sem, wl_sem, wr_sem, wo_sem, wc_sem,
    ms_sem, mr_sem, as_sem, ar_sem, ab_sem, ds_sem, dr_sem,
    xs_sem, xl_sem, xr_sem, xz_sem, o1_sem, o2_sem, lz_sem, rz_sem, f_sem,
):
    me, mp = lax.axis_index("dp"), lax.axis_index("mp")
    core, zh, x = lax.rem(me, 2), lax.rem(lax.div(me, 2), NZH), lax.div(me, 2 * NZH)
    y, zl = lax.rem(mp, NY), lax.div(mp, NY)

    def dpi(a, b, c):
        return (a * NZH + b) * 2 + c

    def at_dp(d):
        return {"dp": d, "mp": mp}

    def at_mp(m):
        return {"dp": me, "mp": m}

    def send(src, dst, ssem, rsem, dev):
        pltpu.make_async_remote_copy(
            src_ref=src, dst_ref=dst, send_sem=ssem, recv_sem=rsem,
            device_id=dev, device_id_type=MESH,
        ).start()

    def await_bytes(view, sem):
        pltpu.make_async_copy(view, view, sem).wait()

    def token_copy(t):
        rows = pl.ds(pl.multiple_of(t * CH, CH), CH)
        return pltpu.make_async_copy(tok_hbm.at[0, rows], tok.at[rows], tok_sem.at[t])

    for t in range(NCH):
        token_copy(t).start()

    barrier = pltpu.get_barrier_semaphore()
    for k in range(1, DP):
        pl.semaphore_signal(barrier, inc=1, device_id=at_dp(lax.rem(me + k, DP)), device_id_type=MESH)
    for k in range(1, MP):
        pl.semaphore_signal(barrier, inc=1, device_id=at_mp(lax.rem(mp + k, MP)), device_id_type=MESH)

    def shard(d):
        return pl.ds(pl.multiple_of(d * SH, SH), SH)

    def part(d):
        return pl.ds(pl.multiple_of(d * 16, 16), 16)

    w[shard(me), :] = wsh[...]
    memg[part(me), :] = memn[...]
    ones = jnp.ones((SEG, HD), BF16)
    vals[:, HD : 2 * HD] = ones
    vals[:, 3 * HD : 4 * HD] = ones
    dacc[...] = jnp.zeros_like(dacc)
    mm[...] = jnp.zeros_like(mm)
    pl.semaphore_wait(barrier, DP - 1 + MP - 1)

    sib = at_dp(me + 1 - 2 * core)
    xp, xm, xo = lax.rem(x + 1, NX), lax.rem(x + 3, NX), lax.rem(x + 2, NX)
    zr = [zh, lax.rem(zh + 3, NZH), lax.rem(zh + 1, NZH), lax.rem(zh + 2, NZH)]
    right, left = at_dp(dpi(xp, zh, core)), at_dp(dpi(xm, zh, core))

    def hand(src, rows):
        send(src, w.at[rows], ws_sem, wc_sem, sib)

    def spread(src, rows, k):
        send(src, w.at[rows], ws_sem, wl_sem.at[k], right)
        send(src, w.at[rows], ws_sem, wr_sem.at[k], left)

    mine = shard(me)
    spread(wsh, mine, 0)
    for k, z_to in ((1, zr[2]), (2, zr[1]), (3, zr[3])):
        send(wsh, w.at[mine], ws_sem, wz_sem.at[k - 1], at_dp(dpi(x, z_to, core)))
    hand(wsh, mine)
    for k in range(1, DP):
        send(memn, memg.at[part(me)], ms_sem, mr_sem, at_dp(lax.rem(me + k, DP)))

    def from_z(k):
        rows = shard(dpi(x, zr[k], core))
        await_bytes(w.at[rows], wz_sem.at[k - 1])
        spread(w.at[rows], rows, k)
        hand(w.at[rows], rows)

    def from_x(k):
        d = dpi(xm, zr[k], core)
        await_bytes(w.at[shard(d)], wl_sem.at[k])
        half = pl.ds(pl.multiple_of(d * SH, SH), SH // 2)
        send(w.at[half], w.at[half], ws_sem, wo_sem.at[k], right)
        hand(w.at[shard(d)], shard(d))
        d = dpi(xp, zr[k], core)
        await_bytes(w.at[shard(d)], wr_sem.at[k])
        half = pl.ds(pl.multiple_of(d * SH + SH // 2, SH // 2), SH // 2)
        send(w.at[half], w.at[half], ws_sem, wo_sem.at[k], left)
        hand(w.at[shard(d)], shard(d))

    def from_opposite(k):
        rows = shard(dpi(xo, zr[k], core))
        await_bytes(w.at[rows], wo_sem.at[k])
        hand(w.at[rows], rows)

    from_x(0)
    from_z(1)
    from_z(2)
    from_opposite(0)
    from_x(1)
    from_x(2)
    from_z(3)
    from_opposite(1)
    from_opposite(2)
    from_x(3)
    from_opposite(3)
    await_bytes(w.at[pl.ds(0, DP // 2 * SH)], wc_sem)

    half_cols = HW // 2
    mine_half = pl.ds(pl.multiple_of(core * half_cols, half_cols), half_cols)
    for k in range(1, MP):
        m = lax.rem(mp + k, MP)
        rows = pl.ds(pl.multiple_of(m * HW + core * half_cols, half_cols), half_cols)
        send(w.at[rows, pl.ds(3 * HW, HW)], wo.at[mp, mine_half], as_sem, ar_sem, at_mp(m))
    wo[mp] = w[pl.ds(pl.multiple_of(mp * HW, HW), HW), pl.ds(3 * HW, HW)]
    seven_halves = wo.at[pl.ds(0, MP - 1), pl.ds(0, half_cols)]

    await_bytes(memg.at[pl.ds(0, (DP - 1) * 16)], mr_sem)
    r = lax.broadcasted_iota(jnp.int32, (HD, DP * 16), 0)
    c = lax.broadcasted_iota(jnp.int32, (HD, DP * 16), 1)
    base = (r >> 2) * 16 + (r & 3)
    for h in range(2):
        for q in range(2):
            pick = (c == base + (h * 4 + q * 8)).astype(F32).astype(BF16)
            mm[h * HD : (h + 1) * HD, q * HW + h * HD : q * HW + (h + 1) * HD] = nn(
                pick, memg[...]
            ).astype(BF16)

    yp = zl * NY + lax.rem(y + 1, NY)
    ym = zl * NY + lax.rem(y + 3, NY)
    yo = zl * NY + lax.rem(y + 2, NY)
    zz = (1 - zl) * NY + y
    zyp = (1 - zl) * NY + lax.rem(y + 1, NY)
    zym = (1 - zl) * NY + lax.rem(y + 3, NY)
    to_yp, to_ym, to_z = at_mp(yp), at_mp(ym), at_mp(zz)

    def piece(m, t, lo, hi):
        return gath.at[m, pl.ds(pl.multiple_of(t * CH + lo, 16), hi - lo)]

    def compute(t):
        token_copy(t).wait()
        rows = pl.ds(pl.multiple_of(t * CH, CH), CH)
        qkv = nn(tok[rows, :], w[:, pl.ds(0, 3 * HW)])
        q, k, v = (qkv[:, i * HW : (i + 1) * HW].astype(BF16) for i in range(3))
        qs[...] = q
        keys[rows, :] = k
        vals[rows, pl.ds(0, HD)] = v[:, :HD]
        vals[rows, pl.ds(2 * HD, HD)] = v[:, HD:]
        fk = feature(k.astype(F32)).astype(BF16)
        rk = nn(fk, mm[...])
        residual = (v.astype(F32) - rk[:, :HW] / rk[:, HW:]).astype(BF16)
        both = jnp.concatenate([residual, jnp.ones((CH, HD), BF16)], axis=1)
        dacc[...] += lax.dot_general(fk, both, (((0,), (0,)), ((), ())), preferred_element_type=F32)

        mx[...] = jnp.full_like(mx, -jnp.inf)
        acc[...] = jnp.zeros_like(acc)

        def score(j, masked):
            cols = pl.ds(pl.multiple_of(j * CH, CH), CH)
            for h in range(2):
                hs = pl.ds(h * HD, HD)
                s = nt(qs[:, hs], keys[cols, hs])
                if masked:
                    a = lax.broadcasted_iota(jnp.int32, (CH, CH), 0)
                    b = lax.broadcasted_iota(jnp.int32, (CH, CH), 1)
                    s = jnp.where(a >= b, s, -1e37)
                scr[h, :, cols] = s
                mx[h] = jnp.maximum(mx[h], jnp.maximum(s[:, :HD], s[:, HD:]))

        @pl.loop(0, t)
        def _(j):
            score(j, False)

        score(t, True)
        top = [jnp.max(mx[h], axis=1, keepdims=True) for h in range(2)]
        for h in range(2):
            mx[h] = jnp.broadcast_to(top[h], (CH, HD))

        @pl.loop(0, t + 1)
        def _(j):
            cols = pl.ds(pl.multiple_of(j * CH, CH), CH)
            for h in range(2):
                m = jnp.concatenate([mx[h], mx[h]], axis=1)
                p = jnp.exp2((scr[h, :, cols] - m) * SCALE2).astype(BF16)
                acc[h] += nn(p, vals[cols, pl.ds(h * HW, HW)])

        fq = feature(qs[...].astype(F32)).astype(BF16)
        rq = nn(fq, mm[...])
        local = jnp.concatenate([acc[h, :, :HD] / acc[h, :, HD:] for h in range(2)], axis=1)
        g = gate[...]
        gath[mp, rows, :] = (g * (rq[:, :HW] / rq[:, HW:]) + (1.0 - g) * local).astype(BF16)

    def first_sends(t):
        own = piece(mp, t, 0, CH)
        send(own, own, xs_sem.at[t], xl_sem.at[t], to_yp)
        send(own, own, xs_sem.at[t], xr_sem.at[t], to_ym)
        send(own, own, xs_sem.at[t], xz_sem.at[t], to_z)

    def pass_on(m, t, lo, hi, rsem, dev):
        send(piece(m, t, lo, hi), piece(m, t, lo, hi), xs_sem.at[t], rsem.at[t], dev)

    def second_sends(t):
        await_bytes(piece(zz, t, 0, CH), xz_sem.at[t])
        pass_on(zz, t, 0, ZF, lz_sem, to_yp)
        pass_on(zz, t, 0, ZF, rz_sem, to_ym)
        await_bytes(piece(ym, t, 0, CH), xl_sem.at[t])
        pass_on(ym, t, L0, L1, o1_sem, to_yp)
        pass_on(ym, t, ZF, CH, f_sem, to_z)
        await_bytes(piece(yp, t, 0, CH), xr_sem.at[t])
        pass_on(yp, t, 0, L0, o2_sem, to_ym)
        pass_on(yp, t, L1, CH, o2_sem, to_ym)
        pass_on(yp, t, ZF, CH, f_sem, to_z)

    def third_sends(t):
        await_bytes(piece(zym, t, 0, ZF), lz_sem.at[t])
        pass_on(zym, t, L0, ZF, f_sem, to_yp)
        await_bytes(piece(zyp, t, 0, ZF), rz_sem.at[t])
        pass_on(zyp, t, 0, L0, f_sem, to_ym)
        await_bytes(piece(yo, t, L0, L1), o1_sem.at[t])
        pass_on(yo, t, ZF, L1, f_sem, to_z)
        await_bytes(piece(yo, t, 0, CH - L1 + L0), o2_sem.at[t])
        pass_on(yo, t, L1, CH, f_sem, to_z)

    last_rows = 3 * (CH - ZF) + ZF

    def project(t):
        await_bytes(gath.at[0, pl.ds(0, last_rows)], f_sem.at[t])
        rows = pl.ds(pl.multiple_of(t * CH, CH), CH)
        total = nt(gath[0, rows, :], wo[0])
        for m in range(1, MP):
            total += nt(gath[m, rows, :], wo[m])
        out[rows, :] = total.astype(BF16)

    def send_updates():
        d = dacc[...].astype(BF16)
        deltas = jnp.concatenate([d[:HD, :HD], d[HD:, HD : 2 * HD]], axis=0)
        sums = d[:, 2 * HD :]
        r = lax.broadcasted_iota(jnp.int32, (DP * 16, HW), 0)
        c = lax.broadcasted_iota(jnp.int32, (DP * 16, HW), 1)
        hit = c == (r >> 4) * 4 + (r & 3) + ((r >> 2) & 1) * HD
        for src, wanted in ((deltas, 0), (sums, 1)):
            pick = (hit & (((r >> 3) & 1) == wanted)).astype(F32).astype(BF16)
            got = nn(pick, src)
            if wanted == 0:
                first = got
        stage[...] = (first + got).astype(BF16)
        drecv[part(me), :] = stage[part(me), :]
        for k in range(1, DP):
            d_to = lax.rem(me + k, DP)
            send(stage.at[part(d_to)], drecv.at[part(me)], ds_sem, dr_sem, at_dp(d_to))

    @pl.loop(0, NCH + 3)
    def _(t):
        @pl.when(t < NCH)
        def _():
            compute(t)
            first_sends(t)

        @pl.when(t == NCH - 1)
        def _():
            send_updates()

        @pl.when((t >= 1) & (t <= NCH))
        def _():
            second_sends(t - 1)

        @pl.when(t == 1)
        def _():
            await_bytes(seven_halves, ar_sem)
            for k in range(1, MP):
                m = lax.rem(mp + k, MP)
                send(wo.at[m, mine_half], wo.at[m, mine_half], as_sem, ab_sem, sib)

        @pl.when((t >= 2) & (t <= NCH + 1))
        def _():
            third_sends(t - 2)

        @pl.when(t == 3)
        def _():
            await_bytes(seven_halves, ab_sem)

        @pl.when(t >= 3)
        def _():
            project(t - 3)

    await_bytes(drecv.at[pl.ds(0, (DP - 1) * 16)], dr_sem)
    total = jnp.sum(drecv[...].astype(F32).reshape(DP, 16, HD), axis=0)
    mem_out[...] = memf[...] + total[:8] / SEG
    norm_out[...] = normf[...] + total[8:] / (SEG * DP)

    await_bytes(w.at[pl.ds(0, 31 * SH)], ws_sem)
    await_bytes(memg.at[pl.ds(0, (DP - 1) * 16)], ms_sem)
    await_bytes(stage.at[pl.ds(0, (DP - 1) * 16)], ds_sem)
    await_bytes(wo.at[pl.ds(0, MP - 1)], as_sem)
    for t in range(NCH):
        await_bytes(gath.at[pl.ds(0, MP - 1), pl.ds(0, CH)], xs_sem.at[t])


def body(tokens, w_query, w_key, w_value, w_out, memory, normalizer, gate_bias):
    wsh = jnp.concatenate([w_query, w_key, w_value, w_out.T], axis=1)
    memf = memory.reshape(8, HD)
    normf = jnp.broadcast_to(normalizer.reshape(8, 1), (8, HD))
    memn = jnp.concatenate([memf, normf], axis=0).astype(BF16)
    gate = jnp.repeat(jax.nn.sigmoid(gate_bias), HD)[None, :]
    dma, vmem = pltpu.SemaphoreType.DMA, pltpu.VMEM
    in_vmem = pl.BlockSpec(memory_space=vmem)
    out, mem_new, norm_new = pl.pallas_call(
        kernel,
        out_shape=(
            jax.ShapeDtypeStruct((SEG, HW), BF16),
            jax.ShapeDtypeStruct((8, HD), F32),
            jax.ShapeDtypeStruct((8, HD), F32),
        ),
        in_specs=[pl.BlockSpec(memory_space=pl.ANY)] + [in_vmem] * 5,
        out_specs=(in_vmem,) * 3,
        scratch_shapes=[
            vmem((SEG, D), BF16),
            vmem((D, PW), BF16),
            vmem((MP, HW, HW), BF16),
            vmem((SEG, HW), BF16),
            vmem((SEG, 2 * HW), BF16),
            vmem((MP, SEG, HW), BF16),
            vmem((CH, HW), BF16),
            vmem((2, CH, SEG), F32),
            vmem((2, CH, HD), F32),
            vmem((2, CH, HW), F32),
            vmem((HW, 2 * HW), BF16),
            vmem((DP * 16, HD), BF16),
            vmem((HW, 3 * HD), F32),
            vmem((DP * 16, HD), BF16),
            vmem((DP * 16, HD), BF16),
            dma((NCH,)), dma, dma((3,)), dma((4,)), dma((4,)), dma((4,)), dma,
            dma, dma, dma, dma, dma, dma, dma,
        ] + [dma((NCH,))] * 9,
        compiler_params=pltpu.CompilerParams(
            collective_id=0, has_side_effects=True, vmem_limit_bytes=58 * 1024 * 1024
        ),
        name="segment_step",
    )(tokens, wsh, memn, memf, normf, gate)
    return (
        out.reshape(1, SEG, HW),
        mem_new.reshape(2, 4, HD),
        norm_new[:, 0].reshape(2, 4),
    )


def solution(mesh):
    in_specs = (
        P("dp", None, None),
        P("dp", "mp"),
        P("dp", "mp"),
        P("dp", "mp"),
        P("mp", "dp"),
        P("mp", "dp", None),
        P("mp", "dp"),
        P("mp"),
    )
    out_specs = (P("dp", None, "mp"), P("mp", "dp", None), P("mp", "dp"))
    return jax.shard_map(body, mesh=mesh, in_specs=in_specs, out_specs=out_specs, check_vma=False)
```

time: 239 us -> 120 us (0.50)
  Pallas kernels: 0 us -> 108 us
  waiting for transfers between devices: 82.1 us -> 0 us
  blocking collectives: 67.6 us -> 0 us
  matrix products: 59.3 us -> 0 us
  between operations: 14 us -> 0.64 us
  other arithmetic: 6.33 us -> 3.49 us
    pallas_call x0 -> x1, Pallas kernels: none -> 108 us  [body(): pl.pallas_call(kernel, out_shape=(jax.ShapeDtypeStruct((SEG, HW), BF16),...]
    reduce_scatter x1 -> x0, waiting for transfers between devices: 73.2 us -> none  [body(): lax.psum_scatter(terms.astype(jnp.float32).astype(jnp.bfloat16), 'mp', sc...]
    all_gather x1 -> x0, blocking collectives: 49.1 us -> none  [in_one_piece_2(): result = lax.all_gather(both, axis, axis=dim, tiled=True)]
    dot_general x12 -> x0, matrix products: 43.2 us -> none  [the longest x4 17.8 us: body(): jnp.einsum('hqk,khd->qhd', probs, value_seq[:last], preferred_element_typ...]
    all_to_all x1 -> x0, blocking collectives: 18.5 us -> none  [sent_and_summed(): tiles = lax.all_to_all(split_up(x, dim, length), axis, 0, 0, tiled=True)]
    sub x4 -> x0, matrix products: 16.2 us -> none  [body(): probs = jax.nn.softmax(scores, axis=-1).astype(jnp.bfloat16)]
    all_gather x2 -> x0, waiting for transfers between devices: 8.16 us -> none  [the longest x1 8.14 us: in_one_piece(): lax.all_gather(both, axis, axis=dim, tiled=True)]
    slice x7 -> x1, local copies, waits for them, and re-layouts: 6.16 us -> 0.79 us  [body(): norm_new[:, 0].reshape(2, 4)]
  transfers between devices with their start and end apart: 3 -> 0, of which waited for: 2 -> 0; matrix products, arithmetic and copies ran while one was open for 28% -> 0% of each run, Pallas kernels for 0% -> 0%
where the time goes in v1:
time: 120 us; the launch traced here: 119 us
  Pallas kernels  108 us (90%)
  local copies, waits for them, and re-layouts  7.1 us (6%)
  other arithmetic  3.49 us (3%)
    pallas_call x1, Pallas kernels, body(): pl.pallas_call(kernel, out_shape=(jax.ShapeDtypeStruct((SEG, HW), BF16),...  108 us
    unnamed x2, local copies, waits for them, and re-layouts  3.53 us

profile of v1, /device:TPU:1, one launch (start us, length us, event | category | flops | bytes accessed | tf_op | source)
XLA Modules:
  0.0 119.2 jit_solution(3544266250273419194)
XLA Ops:
  0.6 0.8 broadcast_in_dim.12
  1.4 0.1 pad.1.clone
  1.5 0.7 add_divide_fusion
  2.1 0.6 broadcast_in_dim.15
  2.8 0.7 convert.7
  3.5 0.7 pad_maximum_fusion.1.memn
  4.1 0.7 broadcast_in_dim.14.normf
  4.8 1.5 %pad_maximum_fusion.wsh = bf16[64,1024]{1,0:T(8,128)(2,1)} fusion(bf16[64,256]{1,0:T(8,128)(2,1)} %bitcast.6, bf16[64,256]{1,0:T(8,128)(2,1)} %param.11, bf16[64,256]{1,0:T(8,128)(2,1)} %param.10, bf16[64,256]{1,0:T(8,128)(2,1)} %param.9), kind=kLoop, calls=%fused_computation | loop fusion | flops 524288 | bytes 262144 | tf_op jit(solution)/shard_map/concatenate | solution.py:344
  6.3 108.0 %segment_step.1 = (bf16[2048,256]{1,0:T(8,128)(2,1)}, f32[8,128]{1,0:T(8,128)}, f32[8,128]{1,0:T(8,128)}) custom-call(bf16[1,2048,2048]{2,1,0:T(8,128)(2,1)} %tok_hbm.1, bf16[64,1024]{1,0:T(8,128)(2,1)} %pad_maximum_fusion.wsh, bf16[16,128]{1,0:T(8,128)(2,1)} %pad_maximum_fusion.1.memn, f32[8,128]{1,0:T(8,128)} %bitcast.8, f32[8,128]{1,0:T(8,128)} %broadcast_in_dim.14.normf, ...), custom_call_target="tpu_custom_call" | custom-call | tf_op jit(solution)/shard_map/segment_step/pallas_call | solution.py:351
  114.2 0.8 slice_reduce_fusion
  115.0 0.6 reshape_squeeze.3
  115.7 2.3 %copy.13 = bf16[1,2048,256]{2,1,0:T(8,128)(2,1)} copy(bf16[1,2048,256]{2,1,0:T(8,128)(2,1)} %bitcast.5) | data formatting | bytes 2097152
  117.9 1.3 %copy.14 = f32[2,4,128]{2,1,0:T(4,128)} copy(f32[2,4,128]{2,1,0:T(4,128)} %bitcast.9) | data formatting | bytes 8192
  (1 shorter events, 0.0 us)
